TPU v7x, 32 devices: a whole 2x2x4 slice. The times are simulated.
32 devices in a mesh: silo: 4 (over z), row: 8 (over y, x, core).
Axes of the slice: x: 2, y: 2, z: 4, core: 2. Of those that a mesh axis runs over, the one named last changes fastest.
Arguments:
- silo_grams: float32 [8, 4096, 4096], P('silo', 'row'), may hold values from -9 to 81, as said below
- silo_weights: bfloat16 [8, 4096, 640], P('silo', 'row'), may hold values from -6 to 6
Outputs:
- merged_rows: float32 [640, 4096], P(('silo', 'row'))
Inputs may be any that keep to these rules, and one draw needn't show every extreme that they name: `silo_grams`: each silo's Gram is symmetric up to float32 rounding and positive definite.
All inputs are finite; a program needn't handle non-finite values.
Results may differ from a plain program's by a relative error of at most 0.0003.
Values may be sent and summed in bfloat16 or wider, within the bound.
No kernel may reach another device: no remote copies, remote signals or barrier semaphores. Data moves between devices by JAX's collectives and lax.ppermute only.
A program may use at most 128 MiB of HBM per device.

v0:
```python
import jax
import jax.numpy as jnp
from jax import lax
from jax.sharding import PartitionSpec as P

ITERS = 2
full_precision = lax.Precision.HIGHEST


def conj_grad(right_side, apply_op, sum_squares, sum_curv):
    solution = jnp.zeros_like(right_side)
    residual = right_side
    direction = right_side
    res_norm = sum_squares(jnp.sum(residual * residual, axis=0))
    for iteration in range(ITERS):
        mapped = apply_op(direction)
        step_size = res_norm / sum_curv(jnp.sum(direction * mapped, axis=0))
        solution = solution + step_size * direction
        residual = residual - step_size * mapped
        if iteration + 1 < ITERS:
            next_norm = sum_squares(jnp.sum(residual * residual, axis=0))
            direction = residual + next_norm / res_norm * direction
            res_norm = next_norm
    return solution


def local(silo_grams, silo_weights):
    partial_op = jnp.sum(silo_grams, axis=0)
    partial_rhs = jnp.einsum(
        "srk,skc->rc",
        silo_grams,
        lax.all_gather(silo_weights, "row", axis=1, tiled=True).astype(jnp.float32),
        precision=full_precision,
    )
    operator = lax.psum(partial_op, "silo")
    right_side = lax.psum_scatter(partial_rhs, "silo", scatter_dimension=1, tiled=True)

    def apply_cols(direction):
        return jnp.dot(
            operator, lax.all_gather(direction, "row", axis=0, tiled=True), precision=full_precision
        )

    def squares_cols(values):
        return lax.psum(values, "row")

    def curv_values(values):
        return lax.psum(values, "row")

    solution = conj_grad(right_side, apply_cols, squares_cols, curv_values)
    transposed = solution.T
    return lax.all_to_all(transposed, "row", split_axis=0, concat_axis=1, tiled=True)


def solution(mesh):
    placed = (P("silo", "row", None), P("silo", "row", None))
    return jax.shard_map(
        local, mesh=mesh, in_specs=placed, out_specs=P(("silo", "row"), None), check_vma=False
    )
```

profile of v0, /device:TPU:0, one launch (start us, length us, event | category | flops | bytes accessed | tf_op | source)
XLA Modules:
  0.0 567.5 jit_solution(10931932025676428913)
XLA Ops:
  6.5 0.0 all-gather.4.cloned.1.call-start
  6.5 2.4 copy.6
  9.0 0.0 all-gather.4.cloned.1.call-update
  9.0 0.0 reduce-scatter.2.cloned.1.call-start
  9.0 68.1 %all-gather.4.cloned.1.call-done = bf16[2,4096,640]{1,2,0:T(8,128)(2,1)} async-done(((bf16[2,512,640]{1,2,0:T(8,128)(2,1)}), bf16[2,4096,640]{1,2,0:T(8,128)(2,1)}) %all-gather.4.cloned.1.call-update) | async-done | bytes 10485776 | tf_op jit(solution)/shard_map/all_gather | solution.py:32
  77.1 21.3 %convolution_bitcast_fusion = f32[512,640]{0,1:T(8,128)} fusion(f32[2,512,4096]{2,1,0:T(8,128)} %param.2, bf16[2,4096,640]{1,2,0:T(8,128)(2,1)} %all-gather.4.cloned.1.call-done), kind=kOutput, calls=%fused_computation | convolution fusion | flops 32212254720 | bytes 28573696 | tf_op jit(solution)/shard_map/srk,skc->rc/dot_general | solution.py:29
  98.4 0.0 reduce-scatter.2.cloned.1.call-update
  98.5 0.0 all-reduce.3.cloned.1.call-start
  98.5 11.6 %reduce_sum.46 = f32[512,4096]{1,0:T(8,128)} reduce(f32[2,512,4096]{2,1,0:T(8,128)} %param.2, f32[]{:T(128)} %constant.0.clone.1), dimensions={0}, to_apply=%region_3.0 | reduce | flops 2097152 | bytes 25165828 | tf_op jit(solution)/shard_map/reduce_sum | solution.py:28
  110.1 0.0 all-reduce.3.cloned.1.call-update
  110.1 0.0 all-gather.6.cloned.1.call-start
  110.2 19.8 %reduce-scatter.2.cloned.1.call-done = f32[512,160]{0,1:T(8,128)} async-done(((f32[512,640]{0,1:T(8,128)}), f32[512,160]{0,1:T(8,128)}) %reduce-scatter.2.cloned.1.call-update) | async-done | bytes 327696 | tf_op jit(solution)/shard_map/reduce_scatter | solution.py:36
  130.0 0.0 copy-start
  130.0 0.0 all-gather.6.cloned.1.call-update
  130.0 0.2 all-gather.8.cloned.1.call-start
  130.2 291.8 %all-reduce.3.cloned.1.call-done = f32[512,4096]{1,0:T(8,128)} async-done(((f32[512,4096]{1,0:T(8,128)}), f32[512,4096]{1,0:T(8,128)}) %all-reduce.3.cloned.1.call-update) | async-done | bytes 8388624 | tf_op jit(solution)/shard_map/psum | solution.py:35
  422.0 30.8 %all-gather.6.cloned.1.call-done = f32[4096,160]{0,1:T(8,128)} async-done(((f32[512,160]{0,1:T(8,128)}), f32[4096,160]{0,1:T(8,128)}) %all-gather.6.cloned.1.call-update) | async-done | bytes 2621456 | tf_op jit(solution)/shard_map/all_gather | solution.py:40
  452.8 13.3 %multiply_reduce_fusion.1 = (f32[160]{0:T(256)S(1)}, f32[160]{0:T(256)S(1)}, f32[512,160]{0,1:T(8,128)S(1)}) fusion(f32[512,160]{0,1:T(8,128)} %reduce-scatter.2.cloned.1.call-done, f32[512,4096]{1,0:T(8,128)} %all-reduce.3.cloned.1.call-done, f32[4096,160]{0,1:T(8,128)} %all-gather.6.cloned.1.call-done), kind=kOutput, calls=%fused_computation.7 | convolution fusion | flops 4026859264 | bytes 11666688 | tf_op jit(solution)/shard_map/dot_general | solution.py:39
  466.0 13.1 %all-reduce = (f32[160]{0:T(256)S(1)}, f32[160]{0:T(256)S(1)}) all-reduce(f32[160]{0:T(256)S(1)} %get-tuple-element.6, f32[160]{0:T(256)S(1)} %get-tuple-element.5), channel_id=1, replica_groups=mesh['silo'=4,'row'=8] {'row'}, use_global_device_ids=true, to_apply=%region_2.0 | all-reduce | flops 320 | bytes 2560 | tf_op jit(solution)/shard_map/psum | solution.py:44
  479.1 0.0 copy-done
  479.1 0.2 multiply_reduce_fusion
  479.3 12.0 %psum.38 = f32[160]{0:T(256)S(1)} all-reduce(f32[160]{0:T(256)S(1)} %multiply_reduce_fusion), channel_id=1, replica_groups=mesh['silo'=4,'row'=8] {'row'}, use_global_device_ids=true, to_apply=%region_8.0 | all-reduce | flops 160 | bytes 1280 | tf_op jit(solution)/shard_map/psum | solution.py:44
  491.4 0.9 multiply_add_fusion
  492.2 0.0 copy-start.1
  492.2 0.0 all-gather.8.cloned.1.call-update
  492.3 30.1 %all-gather.8.cloned.1.call-done = f32[4096,160]{0,1:T(8,128)} async-done(((f32[512,160]{0,1:T(8,128)}), f32[4096,160]{0,1:T(8,128)}) %all-gather.8.cloned.1.call-update) | async-done | bytes 2621456 | tf_op jit(solution)/shard_map/all_gather | solution.py:40
  522.4 13.2 %fusion = f32[160]{0:T(256)S(1)} fusion(f32[512,160]{0,1:T(8,128)} %multiply_add_fusion, f32[512,4096]{1,0:T(8,128)} %all-reduce.3.cloned.1.call-done, f32[4096,160]{0,1:T(8,128)} %all-gather.8.cloned.1.call-done), kind=kOutput, calls=%fused_computation.2 | convolution fusion | flops 4026695680 | bytes 11338368 | tf_op jit(solution)/shard_map/dot_general | solution.py:39
  535.7 13.1 %psum.39 = f32[160]{0:T(256)S(1)} all-reduce(f32[160]{0:T(256)S(1)} %fusion), channel_id=1, replica_groups=mesh['silo'=4,'row'=8] {'row'}, use_global_device_ids=true, to_apply=%region_10.0 | all-reduce | flops 160 | bytes 1280 | tf_op jit(solution)/shard_map/psum | solution.py:47
  548.7 0.0 copy-done.1
  548.8 0.1 add_bitcast_fusion
  548.9 10.9 %all_to_all.19 = f32[8,20,512]{2,1,0:T(8,128)S(1)} all-to-all(f32[8,20,512]{2,1,0:T(8,128)S(1)} %all_to_all.14), channel_id=1, replica_groups=mesh['silo'=4,'row'=8] {'row'}, dimensions={0} | all-to-all | bytes 655360 | tf_op jit(solution)/shard_map/all_to_all | solution.py:51
  559.8 0.2 copy.7
  560.0 1.0 copy.8
  (5 shorter events, 0.1 us)
Async XLA Ops:
  6.5 70.6 %all-gather.4.cloned.1.call-start = ((), (), s32[]{:S(2)}) async-start(), calls=%async_computation.2 | async-start | bytes 11796480 | tf_op jit(solution)/shard_map/all_gather | solution.py:32
  9.0 121.0 %reduce-scatter.2.cloned.1.call-start = ((), (), s32[]{:S(2)}) async-start(), calls=%async_computation.3 | async-start | bytes 1638400 | tf_op jit(solution)/shard_map/reduce_scatter | solution.py:36
  98.5 323.5 %all-reduce.3.cloned.1.call-start = ((), (), s32[]{:S(2)}) async-start(), calls=%async_computation.4 | async-start | bytes 16777216 | tf_op jit(solution)/shard_map/psum | solution.py:35
  110.1 342.7 %all-gather.6.cloned.1.call-start = ((), (), s32[]{:S(2)}) async-start(), calls=%async_computation.5 | async-start | bytes 2949120 | tf_op jit(solution)/shard_map/all_gather | solution.py:40
  130.0 349.2 %copy-start = (f32[512,160]{0,1:T(8,128)S(1)}, f32[512,160]{0,1:T(8,128)}, u32[]{:S(2)}) copy-start(f32[512,160]{0,1:T(8,128)} %reduce-scatter.2.cloned.1.call-done) | copy-start | bytes 983044
  130.0 392.4 %all-gather.8.cloned.1.call-start = ((), (), s32[]{:S(2)}) async-start(), calls=%async_computation.6 | async-start | bytes 2949120 | tf_op jit(solution)/shard_map/all_gather | solution.py:40
  492.2 56.5 %copy-start.1 = (f32[512,160]{0,1:T(8,128)S(1)}, f32[512,160]{0,1:T(8,128)}, u32[]{:S(2)}) copy-start(f32[512,160]{0,1:T(8,128)} %multiply_add_fusion) | copy-start | bytes 983044
Sparse Core Ops, SparseCore 0:
  9.2 67.8 all-gather.3
  98.6 31.3 reduce-scatter.1
  132.5 289.4 all-reduce.2
  423.8 28.9 all-gather.5
  492.4 29.9 all-gather.7
where the time goes:
time: 568 us
  waiting for transfers between devices  441 us (78%)
  blocking collectives  49 us (9%)
  matrix products  47.8 us (8%)
  between operations  13.2 us (2%)
  other arithmetic  12.8 us (2%)
    psum x1, waiting for transfers between devices, local(): operator = lax.psum(partial_op, 'silo')  292 us
    all_gather x1, waiting for transfers between devices, local(): lax.all_gather(silo_weights, 'row', axis=1, tiled=True).astype(jnp.float32)  68.1 us
    all_gather x2, waiting for transfers between devices, apply_cols(): lax.all_gather(direction, 'row', axis=0, tiled=True)  60.9 us
    dot_general x2, matrix products, apply_cols(): jnp.dot(operator, lax.all_gather(direction, 'row', axis=0, tiled=True), p...  26.5 us
    psum x2, blocking collectives, squares_cols(): return lax.psum(values, 'row')  25.1 us
    dot_general x1, matrix products, local(): jnp.einsum('srk,skc->rc', silo_grams, lax.all_gather(silo_weights, 'row',...  21.3 us
    reduce_scatter x1, waiting for transfers between devices, local(): lax.psum_scatter(partial_rhs, 'silo', scatter_dimension=1, tiled=True)  19.8 us
    psum x1, blocking collectives, curv_values(): return lax.psum(values, 'row')  13.1 us
  transfers between devices with their start and end apart: 5, of which 5 were waited for; matrix products, arithmetic and copies ran while one was open for 2% of the time, Pallas kernels for 0%

commit v1 on v0

--- a/solution.py
+++ b/solution.py
@@ -32,7 +32,11 @@
         lax.all_gather(silo_weights, "row", axis=1, tiled=True).astype(jnp.float32),
         precision=full_precision,
     )
-    operator = lax.psum(partial_op, "silo")
+    peers = lax.axis_size("silo")
+    operator, hop = (partial_op, 1)
+    while hop < peers:
+        operator = operator + lax.ppermute(operator, "silo", [(i, i ^ hop) for i in range(peers)])
+        hop = 2 * hop
     right_side = lax.psum_scatter(partial_rhs, "silo", scatter_dimension=1, tiled=True)
 
     def apply_cols(direction):

time: 568 us -> 725 us (1.28)
  waiting for transfers between devices: 441 us -> 571 us
  other arithmetic: 12.8 us -> 35.8 us
    ppermute x0 -> x2, waiting for transfers between devices: none -> 351 us  [local(): lax.ppermute(operator, 'silo', [(i, i ^ hop) for i in range(peers)])]
    psum x1 -> x0, waiting for transfers between devices: 292 us -> none  [local(): operator = lax.psum(partial_op, 'silo')]
    reduce_scatter x1, waiting for transfers between devices: 19.8 us -> 189 us  [local(): lax.psum_scatter(partial_rhs, 'silo', scatter_dimension=1, tiled=True)]
    all_gather x1, waiting for transfers between devices: 68.1 us -> 0.01 us  [local(): lax.all_gather(silo_weights, 'row', axis=1, tiled=True).astype(jnp.float32)]
    all_gather x2, waiting for transfers between devices: 60.9 us -> 30.4 us  [apply_cols(): lax.all_gather(direction, 'row', axis=0, tiled=True)]
    add x0 -> x2, other arithmetic: none -> 22.5 us  [local(): operator + lax.ppermute(operator, 'silo', [(i, i ^ hop) for i in range(pe...]
  transfers between devices with their start and end apart: 5 -> 6, of which waited for: 5 -> 4; matrix products, arithmetic and copies ran while one was open for 2% -> 8% of each run, Pallas kernels for 0% -> 0%
where the time goes in v1:
time: 725 us
  waiting for transfers between devices  571 us (79%)
  blocking collectives  48.7 us (7%)
  matrix products  46.7 us (6%)
  other arithmetic  35.8 us (5%)
  between operations  13.2 us (2%)
    ppermute x2, waiting for transfers between devices, local(): lax.ppermute(operator, 'silo', [(i, i ^ hop) for i in range(peers)])  351 us
    reduce_scatter x1, waiting for transfers between devices, local(): lax.psum_scatter(partial_rhs, 'silo', scatter_dimension=1, tiled=True)  189 us
    all_gather x2, waiting for transfers between devices, apply_cols(): lax.all_gather(direction, 'row', axis=0, tiled=True)  30.4 us
    dot_general x2, matrix products, apply_cols(): jnp.dot(operator, lax.all_gather(direction, 'row', axis=0, tiled=True), p...  25.4 us
    psum x2, blocking collectives, squares_cols(): return lax.psum(values, 'row')  24.8 us
    add x2, other arithmetic, local(): operator + lax.ppermute(operator, 'silo', [(i, i ^ hop) for i in range(pe...  22.5 us
    dot_general x1, matrix products, local(): jnp.einsum('srk,skc->rc', silo_grams, lax.all_gather(silo_weights, 'row',...  21.3 us
  transfers between devices with their start and end apart: 6, of which 4 were waited for; matrix products, arithmetic and copies ran while one was open for 8% of the time, Pallas kernels for 0%

profile of v1, /device:TPU:0, one launch (start us, length us, event | category | flops | bytes accessed | tf_op | source)
XLA Modules:
  0.0 724.5 jit_solution(16021160868798329673)
XLA Ops:
  6.5 0.0 all-gather.4.cloned.1.call-start
  6.5 2.4 copy.6
  9.0 0.0 all-gather.4.cloned.1.call-update
  9.0 0.0 reduce-scatter.2.cloned.1.call-start
  9.0 12.0 %reduce_sum.46 = f32[512,4096]{1,0:T(8,128)} reduce(f32[2,512,4096]{2,1,0:T(8,128)} %param.2, f32[]{:T(128)} %constant.0.clone.1), dimensions={0}, to_apply=%region_3.0 | reduce | flops 2097152 | bytes 25165828 | tf_op jit(solution)/shard_map/reduce_sum | solution.py:28
  21.1 2.8 collective-permute-start
  23.9 180.8 %collective-permute-done = f32[512,4096]{1,0:T(8,128)} collective-permute-done((f32[512,4096]{1,0:T(8,128)}, f32[512,4096]{1,0:T(8,128)}, u32[]{:S(2)}, u32[]{:S(2)}) %collective-permute-start) | collective-permute-done | bytes 8388640 | tf_op jit(solution)/shard_map/ppermute | solution.py:38
  204.7 11.3 %add.22 = f32[512,4096]{1,0:T(8,128)} add(f32[512,4096]{1,0:T(8,128)} %reduce_sum.46, f32[512,4096]{1,0:T(8,128)} %collective-permute-done) | non-fusion elementwise | flops 2097152 | bytes 25165824 | tf_op jit(solution)/shard_map/add | solution.py:38
  216.0 2.7 collective-permute-start.1
  218.7 0.0 all-gather.4.cloned.1.call-done
  218.7 21.3 %convolution_bitcast_fusion = f32[512,640]{0,1:T(8,128)} fusion(f32[2,512,4096]{2,1,0:T(8,128)} %param.2, bf16[2,4096,640]{1,2,0:T(8,128)(2,1)} %all-gather.4.cloned.1.call-done), kind=kOutput, calls=%fused_computation | convolution fusion | flops 32212254720 | bytes 28573696 | tf_op jit(solution)/shard_map/srk,skc->rc/dot_general | solution.py:29
  240.1 0.0 reduce-scatter.2.cloned.1.call-update
  240.1 0.0 all-gather.6.cloned.1.call-start
  240.1 188.8 %reduce-scatter.2.cloned.1.call-done = f32[512,160]{0,1:T(8,128)} async-done(((f32[512,640]{0,1:T(8,128)}), f32[512,160]{0,1:T(8,128)}) %reduce-scatter.2.cloned.1.call-update) | async-done | bytes 327696 | tf_op jit(solution)/shard_map/reduce_scatter | solution.py:40
  428.9 0.0 all-gather.6.cloned.1.call-update
  429.0 0.0 copy-start
  429.0 0.2 all-gather.8.cloned.1.call-start
  429.2 170.5 %collective-permute-done.1 = f32[512,4096]{1,0:T(8,128)} collective-permute-done((f32[512,4096]{1,0:T(8,128)}, f32[512,4096]{1,0:T(8,128)}, u32[]{:S(2)}, u32[]{:S(2)}) %collective-permute-start.1) | collective-permute-done | bytes 8388640 | tf_op jit(solution)/shard_map/ppermute | solution.py:38
  599.7 11.3 %add.23 = f32[512,4096]{1,0:T(8,128)} add(f32[512,4096]{1,0:T(8,128)} %add.22, f32[512,4096]{1,0:T(8,128)} %collective-permute-done.1) | non-fusion elementwise | flops 2097152 | bytes 25165824 | tf_op jit(solution)/shard_map/add | solution.py:38
  611.0 0.0 all-gather.6.cloned.1.call-done
  611.0 0.0 copy-done
  611.0 12.1 %multiply_reduce_fusion.1 = (f32[160]{0:T(256)S(1)}, f32[160]{0:T(256)S(1)}, f32[512,160]{0,1:T(8,128)S(1)}) fusion(f32[512,160]{0,1:T(8,128)S(1)} %copy-done, f32[512,4096]{1,0:T(8,128)} %add.23, f32[4096,160]{0,1:T(8,128)} %all-gather.6.cloned.1.call-done), kind=kOutput, calls=%fused_computation.7 | convolution fusion | flops 4026859264 | bytes 11666688 | tf_op jit(solution)/shard_map/dot_general | solution.py:43
  623.2 12.8 %all-reduce = (f32[160]{0:T(256)S(1)}, f32[160]{0:T(256)S(1)}) all-reduce(f32[160]{0:T(256)S(1)} %get-tuple-element.6, f32[160]{0:T(256)S(1)} %get-tuple-element.5), channel_id=1, replica_groups=mesh['silo'=4,'row'=8] {'row'}, use_global_device_ids=true, to_apply=%region_2.0 | all-reduce | flops 320 | bytes 2560 | tf_op jit(solution)/shard_map/psum | solution.py:48
  635.9 0.2 multiply_reduce_fusion
  636.1 12.0 %psum.30 = f32[160]{0:T(256)S(1)} all-reduce(f32[160]{0:T(256)S(1)} %multiply_reduce_fusion), channel_id=1, replica_groups=mesh['silo'=4,'row'=8] {'row'}, use_global_device_ids=true, to_apply=%region_7.0 | all-reduce | flops 160 | bytes 1280 | tf_op jit(solution)/shard_map/psum | solution.py:48
  648.1 0.9 multiply_add_fusion
  649.0 0.0 copy-start.1
  649.0 0.0 all-gather.8.cloned.1.call-update
  649.0 30.4 %all-gather.8.cloned.1.call-done = f32[4096,160]{0,1:T(8,128)} async-done(((f32[512,160]{0,1:T(8,128)}), f32[4096,160]{0,1:T(8,128)}) %all-gather.8.cloned.1.call-update) | async-done | bytes 2621456 | tf_op jit(solution)/shard_map/all_gather | solution.py:44
  679.4 13.2 %fusion = f32[160]{0:T(256)S(1)} fusion(f32[512,160]{0,1:T(8,128)} %multiply_add_fusion, f32[512,4096]{1,0:T(8,128)} %add.23, f32[4096,160]{0,1:T(8,128)} %all-gather.8.cloned.1.call-done), kind=kOutput, calls=%fused_computation.2 | convolution fusion | flops 4026695680 | bytes 11338368 | tf_op jit(solution)/shard_map/dot_general | solution.py:43
  692.6 13.1 %psum.31 = f32[160]{0:T(256)S(1)} all-reduce(f32[160]{0:T(256)S(1)} %fusion), channel_id=1, replica_groups=mesh['silo'=4,'row'=8] {'row'}, use_global_device_ids=true, to_apply=%region_9.0 | all-reduce | flops 160 | bytes 1280 | tf_op jit(solution)/shard_map/psum | solution.py:51
  705.7 0.0 copy-done.1
  705.7 0.1 add_bitcast_fusion
  705.9 10.9 %all_to_all.19 = f32[8,20,512]{2,1,0:T(8,128)S(1)} all-to-all(f32[8,20,512]{2,1,0:T(8,128)S(1)} %all_to_all.14), channel_id=1, replica_groups=mesh['silo'=4,'row'=8] {'row'}, dimensions={0} | all-to-all | bytes 655360 | tf_op jit(solution)/shard_map/all_to_all | solution.py:55
  716.8 0.2 copy.7
  717.0 1.0 copy.8
  (5 shorter events, 0.1 us)
Async XLA Ops:
  6.5 212.2 %all-gather.4.cloned.1.call-start = ((), (), s32[]{:S(2)}) async-start(), calls=%async_computation.2 | async-start | bytes 11796480 | tf_op jit(solution)/shard_map/all_gather | solution.py:32
  9.0 420.0 %reduce-scatter.2.cloned.1.call-start = ((), (), s32[]{:S(2)}) async-start(), calls=%async_computation.3 | async-start | bytes 1638400 | tf_op jit(solution)/shard_map/reduce_scatter | solution.py:40
  21.1 183.7 %collective-permute-start = (f32[512,4096]{1,0:T(8,128)}, f32[512,4096]{1,0:T(8,128)}, u32[]{:S(2)}, u32[]{:S(2)}) collective-permute-start(f32[512,4096]{1,0:T(8,128)} %reduce_sum.46), channel_id=1, source_target_pairs={{0,8},{8,0},{16,24},{24,16},{1,9},{9,1},{17,25},{25,17},{2,10},{10... | collective-permute-start | bytes 25165832 | tf_op jit(solution)/shard_map/ppermute | solution.py:38
  216.0 383.7 %collective-permute-start.1 = (f32[512,4096]{1,0:T(8,128)}, f32[512,4096]{1,0:T(8,128)}, u32[]{:S(2)}, u32[]{:S(2)}) collective-permute-start(f32[512,4096]{1,0:T(8,128)} %add.22), channel_id=1, source_target_pairs={{0,16},{8,24},{16,0},{24,8},{1,17},{9,25},{17,1},{25,9},{2,18},{10... | collective-permute-start | bytes 25165832 | tf_op jit(solution)/shard_map/ppermute | solution.py:38
  240.1 370.9 %all-gather.6.cloned.1.call-start = ((), (), s32[]{:S(2)}) async-start(), calls=%async_computation.4 | async-start | bytes 2949120 | tf_op jit(solution)/shard_map/all_gather | solution.py:44
  429.0 182.0 %copy-start = (f32[512,160]{0,1:T(8,128)S(1)}, f32[512,160]{0,1:T(8,128)}, u32[]{:S(2)}) copy-start(f32[512,160]{0,1:T(8,128)} %reduce-scatter.2.cloned.1.call-done) | copy-start | bytes 983044
  429.0 250.4 %all-gather.8.cloned.1.call-start = ((), (), s32[]{:S(2)}) async-start(), calls=%async_computation.5 | async-start | bytes 2949120 | tf_op jit(solution)/shard_map/all_gather | solution.py:44
  649.0 56.7 %copy-start.1 = (f32[512,160]{0,1:T(8,128)S(1)}, f32[512,160]{0,1:T(8,128)}, u32[]{:S(2)}) copy-start(f32[512,160]{0,1:T(8,128)} %multiply_add_fusion) | copy-start | bytes 983044
Sparse Core Ops, SparseCore 0:
  9.2 67.8 all-gather.3
  240.2 188.6 reduce-scatter.1
  430.9 32.6 all-gather.5
  649.2 30.1 all-gather.7
